TPU v7x, 32 devices: a whole 2x2x4 slice. The times are simulated.
32 devices in a mesh: groups: 2 (over y), ctx: 4 (over z), role: 2 (over x), seq: 2 (over core).
Axes of the slice: x: 2, y: 2, z: 4, core: 2. Of those that a mesh axis runs over, the one named last changes fastest.
Arguments:
- queries: bfloat16 [32, 128, 576], P(('groups', 'role', 'seq'), 'ctx'), parts along dimension 0, may hold values from -24 to 24
- cache: bfloat16 [16, 4096, 576], P(('groups', 'role', 'seq'), 'ctx'), parts along dimension 0, may hold values from -4 to 4
- lengths: int32 [16], P(('groups', 'role', 'seq')), parts along dimension 0, may hold values from 4 to 4096, as said below
- positions: int32 [32], P(('groups', 'role', 'seq')), parts along dimension 0, may hold values from 0 to 4098, as said below
- value_up_weight: bfloat16 [128, 512, 128], P('ctx', ('role', 'seq')), may hold values from -0.25 to 0.25
- out_proj: bfloat16 [16384, 7168], P('ctx', ('role', 'seq')), may hold values from -0.046875 to 0.046875
- residual: bfloat16 [32, 7168], P('groups', ('role', 'seq')), parts along dimension 0, may hold values from -4 to 4
- norm_gain: float32 [7168], P(('role', 'seq')), may hold values from 0.5 to 1.5
- gate_weight: bfloat16 [7168, 9216], P(('role', 'seq'), 'ctx'), may hold values from -0.0625 to 0.0625
- up_weight: bfloat16 [7168, 9216], P(('role', 'seq'), 'ctx'), may hold values from -0.0625 to 0.0625
- down_weight: bfloat16 [9216, 7168], P('ctx', ('role', 'seq')), may hold values from -0.0625 to 0.0625
Outputs:
- layer_out: bfloat16 [32, 7168], P(('groups', 'ctx'), ('role', 'seq')), parts along dimension 0
There are 2 independent parts, one for each index of `groups`. A program takes and returns all parts, laid end to end along the dimension named above; an argument that names none is the same for every part. Nothing has to cross between parts.
Inputs may be any that keep to these rules, and one draw needn't show every extreme that they name: `lengths`: every sequence has at least 4 cached positions, and in every draw some sequence has all 4096. positions[r] lies between lengths[r // 2] - 4 and lengths[r // 2] + 2.
All inputs are finite; a program needn't handle non-finite values.
Results may differ from a plain program's by a relative error of at most 0.013.
Values may be sent and summed in bfloat16 or wider, within the bound.
A program may use at most 128 MiB of HBM per device.

v0:
```python
import jax
import jax.numpy as jnp
from jax import lax
from jax.sharding import PartitionSpec as P

D = 7168
HEADS = 128
LATENT = 512
ROPE = 64
VDIM = 128
MTP = 2
softmax_scale = 0.07216878364870323
epsilon = 1e-06


def settle_heads(pieces):
    maxima, totals, partial_value = pieces
    highest = jnp.max(maxima, axis=0)
    factor = jnp.exp(maxima - highest[None])
    denom = jnp.sum(factor * totals, axis=0)
    numer = jnp.sum(factor[..., None] * partial_value, axis=0)
    return (numer / denom[..., None]).astype(jnp.bfloat16)


def per_device(
    queries,
    cache,
    lengths,
    positions,
    value_up_weight,
    out_proj,
    residual,
    norm_gain,
    gate_weight,
    up_weight,
    down_weight,
):
    all_heads = lax.all_gather(queries, "ctx", axis=1, tiled=True)
    heads_here = queries.shape[1]
    width = LATENT + ROPE
    context_local = cache.shape[1]
    seq_here = cache.shape[0]
    offset = lax.axis_index("ctx") * context_local
    places = offset + jnp.arange(context_local, dtype=jnp.int32)
    maxima_list = []
    totals_list = []
    partial_list = []
    for number in range(seq_here):
        rows_pair = all_heads[MTP * number : MTP * (number + 1)].reshape(MTP * HEADS, width)
        keys_here = cache[number]
        limits = jnp.repeat(positions[MTP * number : MTP * (number + 1)], HEADS)
        length = lengths[number]

        def compute_block(rows_pair=rows_pair, keys_here=keys_here, limits=limits, length=length):
            scores = (
                jnp.dot(rows_pair, keys_here.T, preferred_element_type=jnp.float32) * softmax_scale
            )
            live = (places[None, :] < length) & (places[None, :] <= limits[:, None])
            block_max = jnp.max(jnp.where(live, scores, jnp.float32(-1e30)), axis=-1)
            probs = jnp.exp(
                jnp.where(live, scores - block_max[:, None], jnp.float32(-1e30))
            ).astype(jnp.bfloat16)
            block_weight_sum = jnp.sum(probs.astype(jnp.float32), axis=-1)
            block_out = jnp.dot(probs, keys_here[:, :LATENT], preferred_element_type=jnp.float32)
            return (block_max, block_weight_sum, block_out)

        block_max, block_weight_sum, block_out = compute_block()
        maxima_list.append(block_max.reshape(MTP, HEADS))
        totals_list.append(block_weight_sum.reshape(MTP, HEADS))
        partial_list.append(block_out.reshape(MTP, HEADS, LATENT))
    maxima = jnp.concatenate(maxima_list, axis=0)
    totals = jnp.concatenate(totals_list, axis=0)
    partial_value = jnp.concatenate(partial_list, axis=0)
    attended_values = settle_heads(
        (
            lax.all_to_all(maxima[None], "ctx", split_axis=2, concat_axis=0, tiled=True),
            lax.all_to_all(totals[None], "ctx", split_axis=2, concat_axis=0, tiled=True),
            lax.all_to_all(partial_value[None], "ctx", split_axis=2, concat_axis=0, tiled=True),
        )
    )
    mixed = jnp.einsum(
        "nut,utc->nuc",
        attended_values,
        lax.all_gather(value_up_weight, ("role", "seq"), axis=1, tiled=True),
        preferred_element_type=jnp.float32,
    )
    value_vectors = mixed.astype(jnp.bfloat16).reshape(attended_values.shape[0], heads_here * VDIM)
    per_head_terms = jnp.dot(
        lax.all_gather(value_vectors, ("role", "seq"), axis=0, tiled=True),
        out_proj,
        preferred_element_type=jnp.float32,
    )
    attn_out = lax.psum(per_head_terms, "ctx")
    resid = residual.astype(jnp.float32) + attn_out
    sumsq = lax.psum(jnp.sum(resid * resid, axis=1), ("role", "seq"))
    normed = (resid * lax.rsqrt(sumsq / D + epsilon)[:, None] * norm_gain[None, :]).astype(
        jnp.bfloat16
    )
    gate_term = jnp.dot(normed, gate_weight, preferred_element_type=jnp.float32)
    up_term = jnp.dot(normed, up_weight, preferred_element_type=jnp.float32)
    gate, up = lax.psum((gate_term, up_term), ("role", "seq"))
    hidden = (jax.nn.silu(gate) * up).astype(jnp.bfloat16)
    rows_here = resid.shape[0] // lax.axis_size("ctx")
    ffn_rows = lax.psum_scatter(
        jnp.dot(hidden, down_weight, preferred_element_type=jnp.float32),
        "ctx",
        scatter_dimension=0,
        tiled=True,
    )
    base_rows = lax.dynamic_slice_in_dim(resid, lax.axis_index("ctx") * rows_here, rows_here, 0)
    return (base_rows + ffn_rows).astype(jnp.bfloat16)


def solution(mesh):
    placed = (
        P(("groups", "role", "seq"), "ctx", None),
        P(("groups", "role", "seq"), "ctx", None),
        P(("groups", "role", "seq")),
        P(("groups", "role", "seq")),
        P("ctx", ("role", "seq"), None),
        P("ctx", ("role", "seq")),
        P("groups", ("role", "seq")),
        P(("role", "seq")),
        P(("role", "seq"), "ctx"),
        P(("role", "seq"), "ctx"),
        P("ctx", ("role", "seq")),
    )
    return jax.shard_map(
        per_device,
        mesh=mesh,
        in_specs=placed,
        out_specs=P(("groups", "ctx"), ("role", "seq")),
        check_vma=False,
    )
```

profile of v0, /device:TPU:0, one launch (start us, length us, event | category | flops | bytes accessed | tf_op | source)
XLA Modules:
  0.0 227.1 jit_solution(11326140525146923370)
XLA Ops:
  6.5 0.0 all-gather.3.cloned.1.call-start
  6.5 0.7 all-gather.3.cloned.1.call-update
  7.3 1.3 fusion.19
  8.6 1.3 fusion.12
  9.9 19.9 %all_gather.9 = bf16[4,128,576]{2,1,0:T(8,128)(2,1)S(1)} all-gather(bf16[4,32,576]{2,1,0:T(8,128)(2,1)} %param.11), channel_id=1, replica_groups=mesh['groups'=2,'ctx'=4,'role'=2,'seq'=2] {'ctx'}, dimensions={1}, use_global_device_ids=true | all-gather | bytes 737280 | tf_op jit(solution)/shard_map/all_gather | solution.py:38
  29.8 0.8 fusion.20
  30.6 0.1 broadcast_bitcast_fusion
  30.7 0.1 fusion.18
  30.7 1.8 convolution_multiply_fusion
  32.6 0.0 copy-done
  32.6 0.9 select_reduce_fusion.1
  33.5 0.9 convert_reduce_fusion.1
  34.4 0.1 copy.23
  34.5 0.6 broadcast.49
  35.1 0.8 reduce.1
  35.9 0.7 reshape.68
  36.6 3.8 %all-to-all-start.2 = ((f32[4,1,128]{2,1,0:T(1,128)}), f32[4,1,128]{2,1,0:T(1,128)S(1)}, u32[]{:S(2)}, u32[]{:S(2)}) async-start(f32[4,1,128]{2,1,0:T(1,128)} %reshape.68), calls=%async_computation.2 | async-start | bytes 4096 | tf_op jit(solution)/shard_map/all_to_all | solution.py:77
  40.4 0.2 slice_bitcast_fusion.1
  40.6 0.5 fusion.3
  41.1 0.5 fusion.1
  41.6 0.1 copy.18
  41.7 0.8 reduce.3
  42.5 0.7 reshape.66
  43.2 0.4 copy.20
  43.6 0.4 copy.21
  44.0 1.9 all-to-all-done.2
  45.9 3.2 %all-to-all-start = ((f32[4,1,128]{2,1,0:T(1,128)}), f32[4,1,128]{2,1,0:T(1,128)S(1)}, u32[]{:S(2)}, u32[]{:S(2)}) async-start(f32[4,1,128]{2,1,0:T(1,128)} %reshape.66), calls=%async_computation | async-start | bytes 4096 | tf_op jit(solution)/shard_map/all_to_all | solution.py:76
  49.1 1.4 maximum_bitcast_fusion
  50.6 4.1 %all-to-all-done = f32[4,1,128]{2,1,0:T(1,128)S(1)} async-done(((f32[4,1,128]{2,1,0:T(1,128)}), f32[4,1,128]{2,1,0:T(1,128)S(1)}, u32[]{:S(2)}, u32[]{:S(2)}) %all-to-all-start) | async-done | bytes 2080 | tf_op jit(solution)/shard_map/all_to_all | solution.py:76
  54.7 3.5 %all-to-all-start.1 = ((f32[1,4,128,512]{3,1,0,2:T(4,128)}), f32[1,4,128,512]{3,1,0,2:T(4,128)S(1)}, u32[]{:S(2)}, u32[]{:S(2)}) async-start(f32[1,4,128,512]{3,1,0,2:T(4,128)} %maximum_bitcast_fusion), calls=%async_computation.1 | async-start | bytes 2097152 | tf_op jit(solution)/shard_map/all_to_all | solution.py:78
  58.2 0.0 all-reduce.6.cloned.1.call-start
  58.3 0.7 reduce.2
  58.9 0.1 reshape.69
  59.1 0.1 copy.24
  59.2 0.7 reduce.4
  59.8 0.1 reshape.67
  60.0 0.1 copy.19
  60.1 18.8 %all-to-all-done.1 = f32[1,4,128,512]{3,1,0,2:T(4,128)S(1)} async-done(((f32[1,4,128,512]{3,1,0,2:T(4,128)}), f32[1,4,128,512]{3,1,0,2:T(4,128)S(1)}, u32[]{:S(2)}, u32[]{:S(2)}) %all-to-all-start.1) | async-done | bytes 1048608 | tf_op jit(solution)/shard_map/all_to_all | solution.py:78
  78.9 0.3 fusion.5
  79.3 0.1 divide_convert_fusion
  79.4 0.0 all-gather.3.cloned.1.call-done
  79.4 2.8 %fusion = bf16[1,4,4096]{2,1,0:T(4,128)(2,1)S(1)} fusion(bf16[32,512,128]{2,1,0:T(8,128)(2,1)} %all-gather.3.cloned.1.call-done, bf16[4,32,512]{2,1,0:T(8,128)(2,1)S(1)} %divide_convert_fusion), kind=kOutput, calls=%fused_computation.5 | convolution fusion | flops 16793600 | bytes 4358144 | tf_op jit(solution)/shard_map/nut,utc->nuc/dot_general | solution.py:81
  82.2 5.4 %all-gather = bf16[4,4,4096]{2,1,0:T(4,128)(2,1)S(1)} all-gather(bf16[1,4,4096]{2,1,0:T(4,128)(2,1)S(1)} %fusion), channel_id=1, replica_groups=mesh['groups'=2,'ctx'=4,'role'=2,'seq'=2] {'role','seq'}, dimensions={0}, use_global_device_ids=true | all-gather | bytes 163840 | tf_op jit(solution)/shard_map/all_gather | solution.py:89
  87.7 0.0 copy-start.2
  87.7 0.0 copy-start.1
  87.7 7.8 %fusion.21 = f32[16,1792]{1,0:T(8,128)} fusion(bf16[16,4096]{1,0:T(8,128)(2,1)S(1)} %reshape.63, bf16[4096,1792]{1,0:T(8,128)(2,1)} %param.16), kind=kOutput, calls=%fused_computation.50 | convolution fusion | flops 234881024 | bytes 14925824 | tf_op jit(solution)/shard_map/dot_general | solution.py:88
  95.5 0.0 all-reduce.6.cloned.1.call-update
  95.6 0.0 all-reduce.10.cloned.1.call-start
  95.6 33.5 %all-reduce.6.cloned.1.call-done = f32[16,1792]{1,0:T(8,128)} async-done(((f32[16,1792]{1,0:T(8,128)}), f32[16,1792]{1,0:T(8,128)}) %all-reduce.6.cloned.1.call-update) | async-done | bytes 114704 | tf_op jit(solution)/shard_map/psum | solution.py:93
  129.1 0.0 copy-done.2
  129.1 1.0 multiply_reduce_fusion
  130.1 5.7 %psum.29 = f32[16]{0:T(128)S(1)} all-reduce(f32[16]{0:T(128)S(1)} %get-tuple-element.9), channel_id=1, replica_groups=mesh['groups'=2,'ctx'=4,'role'=2,'seq'=2] {'role','seq'}, use_global_device_ids=true, to_apply=%region_9.10 | all-reduce | flops 16 | bytes 128 | tf_op jit(solution)/shard_map/psum | solution.py:95
  135.8 0.0 copy-done.1
  135.8 5.2 %fusion.16 = f32[16,2304]{1,0:T(8,128)} fusion(bf16[1792,2304]{1,0:T(8,128)(2,1)} %param.19, f32[16,1792]{1,0:T(8,128)S(1)} %get-tuple-element.10, f32[1792]{0:T(1024)S(1)} %copy-done.1, f32[16]{0:T(128)S(1)} %add_rsqrt_fusion), kind=kOutput, calls=%fused_computation.46 | convolution fusion | flops 132206592 | bytes 8526912 | tf_op jit(solution)/shard_map/dot_general | solution.py:99
  141.1 5.3 %fusion.15 = f32[16,2304]{1,0:T(8,128)} fusion(bf16[1792,2304]{1,0:T(8,128)(2,1)} %param.20, f32[16,1792]{1,0:T(8,128)S(1)} %get-tuple-element.10, f32[1792]{0:T(1024)S(1)} %copy-done.1, f32[16]{0:T(128)S(1)} %add_rsqrt_fusion), kind=kOutput, calls=%fused_computation.45 | convolution fusion | flops 132206592 | bytes 8526912 | tf_op jit(solution)/shard_map/dot_general | solution.py:100
  146.3 0.0 all-reduce.10.cloned.1.call-update
  146.3 0.0 all-reduce.8.cloned.1.call-start
  146.4 32.9 %all-reduce.10.cloned.1.call-done = (f32[16,2304]{1,0:T(8,128)}, f32[16,2304]{1,0:T(8,128)}) async-done(((f32[16,2304]{1,0:T(8,128)}, f32[16,2304]{1,0:T(8,128)}), (f32[16,2304]{1,0:T(8,128)}, f32[16,2304]{1,0:T(8,128)})) %all-reduce.10.cloned.1.call-update) | async-done | bytes 294928 | tf_op jit(solution)/shard_map/psum | solution.py:101
  179.2 5.4 %fusion.7 = f32[16,1792]{1,0:T(8,128)} fusion(bf16[2304,1792]{1,0:T(8,128)(2,1)} %param.21, f32[16,2304]{1,0:T(8,128)} %get-tuple-element.7, f32[16,2304]{1,0:T(8,128)} %get-tuple-element.8), kind=kOutput, calls=%fused_computation.27 | convolution fusion | flops 132341760 | bytes 8667136 | tf_op jit(solution)/shard_map/dot_general | solution.py:105
  184.6 0.0 all-reduce.8.cloned.1.call-update
  184.7 0.0 copy-done.3
  184.7 0.6 dynamic-slice
  185.9 33.3 %all-reduce.8.cloned.1.call-done = f32[16,1792]{1,0:T(8,128)} async-done(((f32[16,1792]{1,0:T(8,128)}), f32[16,1792]{1,0:T(8,128)}) %all-reduce.8.cloned.1.call-update) | async-done | bytes 114704
  219.2 1.4 fusion.9
  (9 shorter events, 0.1 us)
Async XLA Ops:
  6.5 26.1 %copy-start = (bf16[2,1024,576]{1,2,0:T(8,128)(2,1)S(1)}, bf16[2,1024,576]{1,2,0:T(8,128)(2,1)}, u32[]{:S(2)}) copy-start(bf16[2,1024,576]{1,2,0:T(8,128)(2,1)} %param.12) | copy-start | bytes 7077892
  6.5 72.8 %all-gather.3.cloned.1.call-start = ((), (), s32[]{:S(2)}) async-start(), calls=%async_computation.3 | async-start | bytes 5242880 | tf_op jit(solution)/shard_map/all_gather | solution.py:84
  36.6 9.3 %all-to-all-start.2 = ((f32[4,1,128]{2,1,0:T(1,128)}), f32[4,1,128]{2,1,0:T(1,128)S(1)}, u32[]{:S(2)}, u32[]{:S(2)}) async-start(f32[4,1,128]{2,1,0:T(1,128)} %reshape.68), calls=%async_computation.2 | async-start | bytes 4096 | tf_op jit(solution)/shard_map/all_to_all | solution.py:77
  45.9 8.8 %all-to-all-start = ((f32[4,1,128]{2,1,0:T(1,128)}), f32[4,1,128]{2,1,0:T(1,128)S(1)}, u32[]{:S(2)}, u32[]{:S(2)}) async-start(f32[4,1,128]{2,1,0:T(1,128)} %reshape.66), calls=%async_computation | async-start | bytes 4096 | tf_op jit(solution)/shard_map/all_to_all | solution.py:76
  54.7 24.2 %all-to-all-start.1 = ((f32[1,4,128,512]{3,1,0,2:T(4,128)}), f32[1,4,128,512]{3,1,0,2:T(4,128)S(1)}, u32[]{:S(2)}, u32[]{:S(2)}) async-start(f32[1,4,128,512]{3,1,0,2:T(4,128)} %maximum_bitcast_fusion), calls=%async_computation.1 | async-start | bytes 2097152 | tf_op jit(solution)/shard_map/all_to_all | solution.py:78
  58.2 70.9 %all-reduce.6.cloned.1.call-start = ((), (), s32[]{:S(2)}) async-start(), calls=%async_computation.4 | async-start | bytes 229376 | tf_op jit(solution)/shard_map/psum | solution.py:93
  87.7 41.4 %copy-start.2 = (bf16[16,1792]{1,0:T(8,128)(2,1)S(1)}, bf16[16,1792]{1,0:T(8,128)(2,1)}, u32[]{:S(2)}) copy-start(bf16[16,1792]{1,0:T(8,128)(2,1)} %param.17) | copy-start | bytes 172036
  87.7 48.1 %copy-start.1 = (f32[1792]{0:T(1024)S(1)}, f32[1792]{0:T(1024)}, u32[]{:S(2)}) copy-start(f32[1792]{0:T(1024)} %param.18) | copy-start | bytes 21508
  95.6 83.7 %all-reduce.10.cloned.1.call-start = ((), (), s32[]{:S(2)}) async-start(), calls=%async_computation.6 | async-start | bytes 589824 | tf_op jit(solution)/shard_map/psum | solution.py:101
  146.3 72.8 %all-reduce.8.cloned.1.call-start = ((), (), s32[]{:S(2)}) async-start(), calls=%async_computation.5 | async-start | bytes 229376
  179.2 5.4 %copy-start.3 = (u32[32]{0:T(128)S(1)}, u32[32]{0:T(128)}, u32[]{:S(2)}) copy-start(u32[32]{0:T(128)} %constant.35) | copy-start | bytes 388
Sparse Core Ops, SparseCore 0:
  8.9 37.1 all-gather.2
  95.7 33.3 all-reduce.5
  146.4 32.7 all-reduce.9
  184.8 34.3 all-reduce.7
where the time goes:
time: 228 us; the launch traced here: 227 us
  waiting for transfers between devices  125 us (55%)
  blocking collectives  31 us (14%)
  matrix products  30.3 us (13%)
  between operations  14 us (6%)
  starting transfers between devices  10.7 us (5%)
  other arithmetic  9.47 us (4%)
  local copies, waits for them, and re-layouts  6.56 us (3%)
    unnamed x5, waiting for transfers between devices  34 us
    psum x1, waiting for transfers between devices, per_device(): attn_out = lax.psum(per_head_terms, 'ctx')  33.5 us
    psum x1, waiting for transfers between devices, per_device(): gate, up = lax.psum((gate_term, up_term), ('role', 'seq'))  32.9 us
    all_gather x1, blocking collectives, per_device(): all_heads = lax.all_gather(queries, 'ctx', axis=1, tiled=True)  19.9 us
    all_to_all x1, waiting for transfers between devices, per_device(): lax.all_to_all(partial_value[None], 'ctx', split_axis=2, concat_axis=0, t...  18.8 us
    dot_general x1, matrix products, per_device(): jnp.dot(lax.all_gather(value_vectors, ('role', 'seq'), axis=0, tiled=True...  7.84 us
    psum x1, blocking collectives, per_device(): sumsq = lax.psum(jnp.sum(resid * resid, axis=1), ('role', 'seq'))  5.66 us
    all_gather x1, blocking collectives, per_device(): lax.all_gather(value_vectors, ('role', 'seq'), axis=0, tiled=True)  5.41 us
  transfers between devices with their start and end apart: 7, of which 6 were waited for; matrix products, arithmetic and copies ran while one was open for 8% of the time, Pallas kernels for 0%

commit v1 on v0

--- a/solution.py
+++ b/solution.py
@@ -35,7 +35,12 @@
     up_weight,
     down_weight,
 ):
-    all_heads = lax.all_gather(queries, "ctx", axis=1, tiled=True)
+    ring = [queries]
+    for hop in range(3):
+        ring.append(lax.ppermute(ring[-1], "ctx", [(dev, (dev + 1) % 4) for dev in range(4)]))
+    all_heads = jnp.roll(
+        jnp.concatenate(ring[::-1], axis=1), (lax.axis_index("ctx") + 1) * ring[0].shape[1], axis=1
+    )
     heads_here = queries.shape[1]
     width = LATENT + ROPE
     context_local = cache.shape[1]

time: 228 us -> 231 us (1.013)
  blocking collectives: 31 us -> 11.1 us
  waiting for transfers between devices: 125 us -> 141 us
  starting transfers between devices: 10.7 us -> 14.9 us
  local copies, waits for them, and re-layouts: 6.56 us -> 8.93 us
    all_gather x1 -> x0, blocking collectives: 19.9 us -> none  [per_device(): all_heads = lax.all_gather(queries, 'ctx', axis=1, tiled=True)]
    ppermute x0 -> x3, waiting for transfers between devices: none -> 16.8 us  [per_device(): lax.ppermute(ring[-1], 'ctx', [(dev, (dev + 1) % 4) for dev in range(4)])]
    all_to_all x1, waiting for transfers between devices: 4.12 us -> 0.1 us  [per_device(): lax.all_to_all(maxima[None], 'ctx', split_axis=2, concat_axis=0, tiled=True)]
    ppermute x0 -> x3, starting transfers between devices: none -> 3.11 us  [per_device(): lax.ppermute(ring[-1], 'ctx', [(dev, (dev + 1) % 4) for dev in range(4)])]
    unnamed x15 -> x34, local copies, waits for them, and re-layouts: 2.89 us -> 5.05 us
  transfers between devices with their start and end apart: 7 -> 10, of which waited for: 6 -> 9; matrix products, arithmetic and copies ran while one was open for 8% -> 8% of each run, Pallas kernels for 0% -> 0%
where the time goes in v1:
time: 231 us; the launch traced here: 230 us
  waiting for transfers between devices  141 us (61%)
  matrix products  29.9 us (13%)
  starting transfers between devices  14.9 us (6%)
  between operations  14.1 us (6%)
  blocking collectives  11.1 us (5%)
  other arithmetic  10.4 us (5%)
  local copies, waits for them, and re-layouts  8.93 us (4%)
    unnamed x5, waiting for transfers between devices  34 us
    psum x1, waiting for transfers between devices, per_device(): attn_out = lax.psum(per_head_terms, 'ctx')  33 us
    psum x1, waiting for transfers between devices, per_device(): gate, up = lax.psum((gate_term, up_term), ('role', 'seq'))  32.9 us
    all_to_all x1, waiting for transfers between devices, per_device(): lax.all_to_all(partial_value[None], 'ctx', split_axis=2, concat_axis=0, t...  19.9 us
    ppermute x3, waiting for transfers between devices, per_device(): lax.ppermute(ring[-1], 'ctx', [(dev, (dev + 1) % 4) for dev in range(4)])  16.8 us
    dot_general x1, matrix products, per_device(): jnp.dot(lax.all_gather(value_vectors, ('role', 'seq'), axis=0, tiled=True...  7.84 us
    psum x1, blocking collectives, per_device(): sumsq = lax.psum(jnp.sum(resid * resid, axis=1), ('role', 'seq'))  5.66 us
    all_gather x1, blocking collectives, per_device(): lax.all_gather(value_vectors, ('role', 'seq'), axis=0, tiled=True)  5.41 us
  transfers between devices with their start and end apart: 10, of which 9 were waited for; matrix products, arithmetic and copies ran while one was open for 8% of the time, Pallas kernels for 0%

profile of v1, /device:TPU:0, one launch (start us, length us, event | category | flops | bytes accessed | tf_op | source)
XLA Modules:
  0.0 230.1 jit_solution(6211619310496948453)
XLA Ops:
  6.5 0.7 all-gather.3.cloned.1.call-update
  7.3 3.1 %collective-permute-start = (bf16[4,32,576]{2,1,0:T(8,128)(2,1)}, bf16[4,32,576]{2,1,0:T(8,128)(2,1)S(1)}, u32[]{:S(2)}, u32[]{:S(2)}) collective-permute-start(bf16[4,32,576]{2,1,0:T(8,128)(2,1)} %param.11), channel_id=1, source_target_pairs={{0,4},{4,8},{8,12},{12,0},{1,5},{5,9},{9,13},{13,1},{2,6},{6,10},{... | collective-permute-start | bytes 442376 | tf_op jit(solution)/shard_map/ppermute | solution.py:40
  10.4 1.8 slice_bitcast_fusion.1
  12.2 0.1 fusion.19
  12.3 4.5 %collective-permute-done = bf16[4,32,576]{2,1,0:T(8,128)(2,1)S(1)} collective-permute-done((bf16[4,32,576]{2,1,0:T(8,128)(2,1)}, bf16[4,32,576]{2,1,0:T(8,128)(2,1)S(1)}, u32[]{:S(2)}, u32[]{:S(2)}) %collective-permute-start) | collective-permute-done | bytes 147488 | tf_op jit(solution)/shard_map/ppermute | solution.py:40
  16.8 0.1 broadcast_bitcast_fusion
  16.9 0.6 fusion.18
  17.5 6.5 %collective-permute-done.1 = bf16[4,32,576]{2,1,0:T(8,128)(2,1)S(1)} collective-permute-done((bf16[4,32,576]{2,1,0:T(8,128)(2,1)S(1)}, bf16[4,32,576]{2,1,0:T(8,128)(2,1)S(1)}, u32[]{:S(2)}, u32[]{:S(2)}) %collective-permute-start.1) | collective-permute-done | bytes 147488 | tf_op jit(solution)/shard_map/ppermute | solution.py:40
  24.0 1.3 fusion.12
  25.3 5.8 %collective-permute-done.2 = bf16[4,32,576]{2,1,0:T(8,128)(2,1)S(1)} collective-permute-done((bf16[4,32,576]{2,1,0:T(8,128)(2,1)S(1)}, bf16[4,32,576]{2,1,0:T(8,128)(2,1)S(1)}, u32[]{:S(2)}, u32[]{:S(2)}) %collective-permute-start.2) | collective-permute-done | bytes 147488 | tf_op jit(solution)/shard_map/ppermute | solution.py:40
  31.4 0.1 constant_dynamic-slice_fusion
  31.4 1.5 copy-done
  32.9 0.6 convolution_multiply_fusion
  33.5 1.8 select_reduce_fusion.1
  35.3 0.6 copy-done.5
  35.9 0.0 copy-done.6
  35.9 0.1 copy.18
  36.0 0.5 broadcast.50
  36.5 0.7 reduce.3
  37.3 0.7 reshape.66
  38.0 3.2 %all-to-all-start = ((f32[4,1,128]{2,1,0:T(1,128)}), f32[4,1,128]{2,1,0:T(1,128)S(1)}, u32[]{:S(2)}, u32[]{:S(2)}) async-start(f32[4,1,128]{2,1,0:T(1,128)} %reshape.66), calls=%async_computation | async-start | bytes 4096 | tf_op jit(solution)/shard_map/all_to_all | solution.py:81
  41.2 2.1 convert_reduce_fusion.1
  43.3 0.5 fusion.3
  43.7 0.5 fusion.1
  44.2 0.1 copy.23
  44.4 0.7 reduce.1
  45.1 0.7 reshape.68
  45.8 0.4 copy.20
  46.2 0.4 copy.21
  46.6 0.1 all-to-all-done
  46.7 5.0 %all-to-all-start.2 = ((f32[4,1,128]{2,1,0:T(1,128)}), f32[4,1,128]{2,1,0:T(1,128)S(1)}, u32[]{:S(2)}, u32[]{:S(2)}) async-start(f32[4,1,128]{2,1,0:T(1,128)} %reshape.68), calls=%async_computation.2 | async-start | bytes 4096 | tf_op jit(solution)/shard_map/all_to_all | solution.py:82
  51.7 1.4 maximum_bitcast_fusion
  53.1 4.0 %all-to-all-done.2 = f32[4,1,128]{2,1,0:T(1,128)S(1)} async-done(((f32[4,1,128]{2,1,0:T(1,128)}), f32[4,1,128]{2,1,0:T(1,128)S(1)}, u32[]{:S(2)}, u32[]{:S(2)}) %all-to-all-start.2) | async-done | bytes 2080 | tf_op jit(solution)/shard_map/all_to_all | solution.py:82
  57.2 3.5 %all-to-all-start.1 = ((f32[1,4,128,512]{3,1,0,2:T(4,128)}), f32[1,4,128,512]{3,1,0,2:T(4,128)S(1)}, u32[]{:S(2)}, u32[]{:S(2)}) async-start(f32[1,4,128,512]{3,1,0,2:T(4,128)} %maximum_bitcast_fusion), calls=%async_computation.1 | async-start | bytes 2097152 | tf_op jit(solution)/shard_map/all_to_all | solution.py:83
  60.7 0.0 all-reduce.6.cloned.1.call-start
  60.8 0.6 reduce.4
  61.3 0.1 reshape.67
  61.5 0.1 copy.19
  61.6 0.6 reduce.2
  62.2 0.1 reshape.69
  62.3 0.1 copy.24
  62.5 19.9 %all-to-all-done.1 = f32[1,4,128,512]{3,1,0,2:T(4,128)S(1)} async-done(((f32[1,4,128,512]{3,1,0,2:T(4,128)}), f32[1,4,128,512]{3,1,0,2:T(4,128)S(1)}, u32[]{:S(2)}, u32[]{:S(2)}) %all-to-all-start.1) | async-done | bytes 1048608 | tf_op jit(solution)/shard_map/all_to_all | solution.py:83
  82.4 0.3 fusion.5
  82.7 0.1 divide_convert_fusion
  82.8 0.0 all-gather.3.cloned.1.call-done
  82.8 2.8 %fusion = bf16[1,4,4096]{2,1,0:T(4,128)(2,1)S(1)} fusion(bf16[32,512,128]{2,1,0:T(8,128)(2,1)} %all-gather.3.cloned.1.call-done, bf16[4,32,512]{2,1,0:T(8,128)(2,1)S(1)} %divide_convert_fusion), kind=kOutput, calls=%fused_computation.5 | convolution fusion | flops 16793600 | bytes 4358144 | tf_op jit(solution)/shard_map/nut,utc->nuc/dot_general | solution.py:86
  85.7 5.4 %all-gather = bf16[4,4,4096]{2,1,0:T(4,128)(2,1)S(1)} all-gather(bf16[1,4,4096]{2,1,0:T(4,128)(2,1)S(1)} %fusion), channel_id=1, replica_groups=mesh['groups'=2,'ctx'=4,'role'=2,'seq'=2] {'role','seq'}, dimensions={0}, use_global_device_ids=true | all-gather | bytes 163840 | tf_op jit(solution)/shard_map/all_gather | solution.py:94
  91.1 0.0 copy-start.3
  91.1 7.8 %fusion.20 = f32[16,1792]{1,0:T(8,128)} fusion(bf16[16,4096]{1,0:T(8,128)(2,1)S(1)} %reshape.63, bf16[4096,1792]{1,0:T(8,128)(2,1)} %param.16), kind=kOutput, calls=%fused_computation.59 | convolution fusion | flops 234881024 | bytes 14925824 | tf_op jit(solution)/shard_map/dot_general | solution.py:93
  99.0 0.0 all-reduce.6.cloned.1.call-update
  99.0 0.0 all-reduce.10.cloned.1.call-start
  99.0 33.0 %all-reduce.6.cloned.1.call-done = f32[16,1792]{1,0:T(8,128)} async-done(((f32[16,1792]{1,0:T(8,128)}), f32[16,1792]{1,0:T(8,128)}) %all-reduce.6.cloned.1.call-update) | async-done | bytes 114704 | tf_op jit(solution)/shard_map/psum | solution.py:98
  132.1 1.0 multiply_reduce_fusion
  133.1 5.7 %psum.29 = f32[16]{0:T(128)S(1)} all-reduce(f32[16]{0:T(128)S(1)} %get-tuple-element.9), channel_id=1, replica_groups=mesh['groups'=2,'ctx'=4,'role'=2,'seq'=2] {'role','seq'}, use_global_device_ids=true, to_apply=%region_9.10 | all-reduce | flops 16 | bytes 128 | tf_op jit(solution)/shard_map/psum | solution.py:100
  138.8 5.2 %fusion.16 = f32[16,2304]{1,0:T(8,128)} fusion(bf16[1792,2304]{1,0:T(8,128)(2,1)} %param.19, f32[16,1792]{1,0:T(8,128)S(1)} %get-tuple-element.10, f32[1792]{0:T(1024)S(1)} %copy-done.2, f32[16]{0:T(128)S(1)} %add_rsqrt_fusion), kind=kOutput, calls=%fused_computation.56 | convolution fusion | flops 132206592 | bytes 8526912 | tf_op jit(solution)/shard_map/dot_general | solution.py:104
  144.0 5.3 %fusion.15 = f32[16,2304]{1,0:T(8,128)} fusion(bf16[1792,2304]{1,0:T(8,128)(2,1)} %param.20, f32[16,1792]{1,0:T(8,128)S(1)} %get-tuple-element.10, f32[1792]{0:T(1024)S(1)} %copy-done.2, f32[16]{0:T(128)S(1)} %add_rsqrt_fusion), kind=kOutput, calls=%fused_computation.55 | convolution fusion | flops 132206592 | bytes 8526912 | tf_op jit(solution)/shard_map/dot_general | solution.py:105
  149.3 0.0 all-reduce.10.cloned.1.call-update
  149.3 0.0 all-reduce.8.cloned.1.call-start
  149.3 32.9 %all-reduce.10.cloned.1.call-done = (f32[16,2304]{1,0:T(8,128)}, f32[16,2304]{1,0:T(8,128)}) async-done(((f32[16,2304]{1,0:T(8,128)}, f32[16,2304]{1,0:T(8,128)}), (f32[16,2304]{1,0:T(8,128)}, f32[16,2304]{1,0:T(8,128)})) %all-reduce.10.cloned.1.call-update) | async-done | bytes 294928 | tf_op jit(solution)/shard_map/psum | solution.py:106
  182.2 5.4 %fusion.7 = f32[16,1792]{1,0:T(8,128)} fusion(bf16[2304,1792]{1,0:T(8,128)(2,1)} %param.21, f32[16,2304]{1,0:T(8,128)} %get-tuple-element.7, f32[16,2304]{1,0:T(8,128)} %get-tuple-element.8), kind=kOutput, calls=%fused_computation.27 | convolution fusion | flops 132341760 | bytes 8667136 | tf_op jit(solution)/shard_map/dot_general | solution.py:110
  187.6 0.0 all-reduce.8.cloned.1.call-update
  187.6 0.6 dynamic-slice
  188.9 33.3 %all-reduce.8.cloned.1.call-done = f32[16,1792]{1,0:T(8,128)} async-done(((f32[16,1792]{1,0:T(8,128)}), f32[16,1792]{1,0:T(8,128)}) %all-reduce.8.cloned.1.call-update) | async-done | bytes 114704
  222.1 1.4 fusion.9
  (34 shorter events, 0.3 us)
Async XLA Ops:
  6.5 76.3 %all-gather.3.cloned.1.call-start = ((), (), s32[]{:S(2)}) async-start(), calls=%async_computation.3 | async-start | bytes 5242880 | tf_op jit(solution)/shard_map/all_gather | solution.py:89
  7.3 5.0 %copy-start.7 = (s32[4]{0:T(128)S(1)}, s32[4]{0:T(128)}, u32[]{:S(2)}) copy-start(s32[4]{0:T(128)} %param.14) | copy-start | bytes 52
  7.3 9.6 %copy-start.8 = (s32[2]{0:T(128)S(1)}, s32[2]{0:T(128)}, u32[]{:S(2)}) copy-start(s32[2]{0:T(128)} %param.13) | copy-start | bytes 28
  7.3 23.9 %copy-start.1 = (bf16[4,32,576]{2,1,0:T(8,128)(2,1)S(1)}, bf16[4,32,576]{2,1,0:T(8,128)(2,1)}, u32[]{:S(2)}) copy-start(bf16[4,32,576]{2,1,0:T(8,128)(2,1)} %param.11) | copy-start | bytes 442372
  7.3 9.5 %collective-permute-start = (bf16[4,32,576]{2,1,0:T(8,128)(2,1)}, bf16[4,32,576]{2,1,0:T(8,128)(2,1)S(1)}, u32[]{:S(2)}, u32[]{:S(2)}) collective-permute-start(bf16[4,32,576]{2,1,0:T(8,128)(2,1)} %param.11), channel_id=1, source_target_pairs={{0,4},{4,8},{8,12},{12,0},{1,5},{5,9},{9,13},{13,1},{2,6},{6,10},{... | collective-permute-start | bytes 442376 | tf_op jit(solution)/shard_map/ppermute | solution.py:40
  16.8 7.2 %collective-permute-start.1 = (bf16[4,32,576]{2,1,0:T(8,128)(2,1)S(1)}, bf16[4,32,576]{2,1,0:T(8,128)(2,1)S(1)}, u32[]{:S(2)}, u32[]{:S(2)}) collective-permute-start(bf16[4,32,576]{2,1,0:T(8,128)(2,1)S(1)} %collective-permute-done), channel_id=1, source_target_pairs={{0,4},{4,8},{8,12},{12,0},{1,5},{5,9},{9,13},{13,1},{2,6},{6,10},{... | collective-permute-start | bytes 442376 | tf_op jit(solution)/shard_map/ppermute | solution.py:40
  24.0 7.1 %collective-permute-start.2 = (bf16[4,32,576]{2,1,0:T(8,128)(2,1)S(1)}, bf16[4,32,576]{2,1,0:T(8,128)(2,1)S(1)}, u32[]{:S(2)}, u32[]{:S(2)}) collective-permute-start(bf16[4,32,576]{2,1,0:T(8,128)(2,1)S(1)} %collective-permute-done.1), channel_id=1, source_target_pairs={{0,4},{4,8},{8,12},{12,0},{1,5},{5,9},{9,13},{13,1},{2,6},{6,10},{... | collective-permute-start | bytes 442376 | tf_op jit(solution)/shard_map/ppermute | solution.py:40
  25.3 8.2 %copy-start.4 = (pred[1024]{0:T(1024)(128)(4,1)}, pred[1024]{0:T(1024)(128)(4,1)S(1)}, u32[]{:S(2)}) copy-start(pred[1024]{0:T(1024)(128)(4,1)S(1)} %get-tuple-element.29) | copy-start | bytes 3076
  31.2 1.7 copy-start
  35.3 0.6 copy-start.5
  35.3 0.6 copy-start.6
  38.0 8.7 %all-to-all-start = ((f32[4,1,128]{2,1,0:T(1,128)}), f32[4,1,128]{2,1,0:T(1,128)S(1)}, u32[]{:S(2)}, u32[]{:S(2)}) async-start(f32[4,1,128]{2,1,0:T(1,128)} %reshape.66), calls=%async_computation | async-start | bytes 4096 | tf_op jit(solution)/shard_map/all_to_all | solution.py:81
  46.7 10.5 %all-to-all-start.2 = ((f32[4,1,128]{2,1,0:T(1,128)}), f32[4,1,128]{2,1,0:T(1,128)S(1)}, u32[]{:S(2)}, u32[]{:S(2)}) async-start(f32[4,1,128]{2,1,0:T(1,128)} %reshape.68), calls=%async_computation.2 | async-start | bytes 4096 | tf_op jit(solution)/shard_map/all_to_all | solution.py:82
  57.2 25.2 %all-to-all-start.1 = ((f32[1,4,128,512]{3,1,0,2:T(4,128)}), f32[1,4,128,512]{3,1,0,2:T(4,128)S(1)}, u32[]{:S(2)}, u32[]{:S(2)}) async-start(f32[1,4,128,512]{3,1,0,2:T(4,128)} %maximum_bitcast_fusion), calls=%async_computation.1 | async-start | bytes 2097152 | tf_op jit(solution)/shard_map/all_to_all | solution.py:83
  60.7 71.3 %all-reduce.6.cloned.1.call-start = ((), (), s32[]{:S(2)}) async-start(), calls=%async_computation.4 | async-start | bytes 229376 | tf_op jit(solution)/shard_map/psum | solution.py:98
  91.1 40.9 %copy-start.3 = (bf16[16,1792]{1,0:T(8,128)(2,1)S(1)}, bf16[16,1792]{1,0:T(8,128)(2,1)}, u32[]{:S(2)}) copy-start(bf16[16,1792]{1,0:T(8,128)(2,1)} %param.17) | copy-start | bytes 172036
  91.1 47.6 %copy-start.2 = (f32[1792]{0:T(1024)S(1)}, f32[1792]{0:T(1024)}, u32[]{:S(2)}) copy-start(f32[1792]{0:T(1024)} %param.18) | copy-start | bytes 21508
  99.0 83.2 %all-reduce.10.cloned.1.call-start = ((), (), s32[]{:S(2)}) async-start(), calls=%async_computation.6 | async-start | bytes 589824 | tf_op jit(solution)/shard_map/psum | solution.py:106
  149.3 72.8 %all-reduce.8.cloned.1.call-start = ((), (), s32[]{:S(2)}) async-start(), calls=%async_computation.5 | async-start | bytes 229376
  182.2 5.4 %copy-start.9 = (u32[32]{0:T(128)S(1)}, u32[32]{0:T(128)}, u32[]{:S(2)}) copy-start(u32[32]{0:T(128)} %constant.60) | copy-start | bytes 388
Sparse Core Ops, SparseCore 0:
  8.9 37.1 all-gather.2
  99.1 32.8 all-reduce.5
  149.4 32.7 all-reduce.9
  187.7 34.3 all-reduce.7
